TPU v7x, 32 devices: a whole 2x2x4 slice. The times are simulated.
32 devices in a mesh: prow: 8 (over z, y), pcol: 4 (over x, core).
Axes of the slice: x: 2, y: 2, z: 4, core: 2. Of those that a mesh axis runs over, the one named last changes fastest.
Arguments:
- inverse_block: bfloat16 [2, 512, 512], P(None, 'prow', 'pcol'), may hold values from -1.75 to 1.75
- panel: bfloat16 [2, 512, 2048], P(None, ('prow', 'pcol')), may hold values from -0.5 to 0.5
- pattern: int32 [1, 4], replicated, may hold values 0 or 1
- diag_inverse: float32 [2, 512, 2048], P(None, None, 'pcol'), may hold values from -6 to 6
Outputs:
- offdiag: bfloat16 [2, 512, 2048], P(None, 'prow', 'pcol')
- diagonal: float32 [2, 512, 2048], P(None, None, 'pcol')
All inputs are finite; a program needn't handle non-finite values.
Results may differ from a plain program's by a relative error of at most 0.0024.
Values may be sent and summed in bfloat16 or wider, within the bound.
A program may use at most 64 MiB of HBM per device.

v0:
```python
import jax
import jax.numpy as jnp
from jax import lax
from jax.sharding import PartitionSpec as P

WIDTH = 512


def complex_product(left_real, left_imag, right_real, right_imag, contract):
    dims = (((contract,), (0,)), ((), ()))
    real_part = lax.dot_general(
        left_real, right_real, dims, preferred_element_type=jnp.float32
    ) - lax.dot_general(left_imag, right_imag, dims, preferred_element_type=jnp.float32)
    imag_part = lax.dot_general(
        left_real, right_imag, dims, preferred_element_type=jnp.float32
    ) + lax.dot_general(left_imag, right_real, dims, preferred_element_type=jnp.float32)
    return (real_part, imag_part)


def keep_table(pattern, row_start, row_count, col_start, col_count, block_width):
    row_ids = (row_start + jnp.arange(row_count, dtype=jnp.int32)) // block_width
    col_ids = (col_start + jnp.arange(col_count, dtype=jnp.int32)) // block_width
    row_select = (
        row_ids[:, None] == jnp.arange(pattern.shape[0], dtype=jnp.int32)[None, :]
    ).astype(jnp.float32)
    col_select = (
        col_ids[:, None] == jnp.arange(pattern.shape[1], dtype=jnp.int32)[None, :]
    ).astype(jnp.float32)
    pattern_value = pattern.astype(jnp.float32)
    row_pattern = jnp.dot(row_select, pattern_value, precision=lax.Precision.HIGHEST)
    return jnp.dot(row_pattern, col_select.T, precision=lax.Precision.HIGHEST)


def local(inverse_block, panel, pattern, diag_inverse):
    rows_dev = inverse_block.shape[1]
    block_span = inverse_block.shape[2]
    fine_rows = panel.shape[1]
    columns = panel.shape[2]
    row_index = lax.axis_index("prow")
    col_index = lax.axis_index("pcol")
    col_count = lax.axis_size("pcol")
    root_count = lax.axis_size("prow") // col_count
    fine_start = (row_index * col_count + col_index) * fine_rows
    keep_mask = keep_table(pattern, fine_start, fine_rows, 0, columns, WIDTH)
    masked = jnp.where(keep_mask[None] > 0.5, panel, jnp.zeros_like(panel))
    row_panel = lax.all_gather(masked, "pcol", axis=1, tiled=True)
    flipped = jnp.swapaxes(inverse_block, 1, 2)
    split_cols = flipped.reshape(2, root_count, col_count, fine_rows, rows_dev)
    received = lax.all_to_all(split_cols, "pcol", split_axis=2, concat_axis=1, tiled=True)
    regrouped = received.reshape(2, block_span, rows_dev)
    panel_piece = lax.all_gather(masked, "prow", axis=1, tiled=True)
    part_real, part_imag = complex_product(
        regrouped[0], regrouped[1], panel_piece[0], panel_piece[1], 0
    )
    stacked = jnp.stack([part_real, part_imag])
    summed = lax.psum_scatter(stacked, "pcol", scatter_dimension=2, tiled=True)
    local_cols = summed.shape[2]
    keep_local = keep_table(
        pattern, row_index * rows_dev, rows_dev, col_index * local_cols, local_cols, WIDTH
    )
    coupled = (summed * keep_local[None]).astype(jnp.bfloat16)
    offdiag = -coupled
    block_start = col_index * local_cols // WIDTH * WIDTH
    lower_panel = lax.dynamic_slice_in_dim(row_panel, block_start, WIDTH, 2)
    diag_real, diag_imag = complex_product(
        lower_panel[0], lower_panel[1], coupled[0], coupled[1], 0
    )
    shares = lax.psum_scatter(
        jnp.stack([diag_real, diag_imag]), "prow", scatter_dimension=1, tiled=True
    )
    correction = lax.all_gather(shares, "prow", axis=1, tiled=True)
    return (offdiag, diag_inverse + correction)


def solution(mesh):
    in_specs = (
        P(None, "prow", "pcol"),
        P(None, ("prow", "pcol"), None),
        P(),
        P(None, None, "pcol"),
    )
    out_specs = (P(None, "prow", "pcol"), P(None, None, "pcol"))
    return jax.shard_map(local, mesh=mesh, in_specs=in_specs, out_specs=out_specs, check_vma=False)
```

profile of v0, /device:TPU:1, one launch (start us, length us, event | category | flops | bytes accessed | tf_op | source)
XLA Modules:
  0.0 212.2 jit_solution(16898340930722284187)
XLA Ops:
  7.2 0.0 all-gather.3.cloned.1.call-start
  7.2 0.7 convert_bitcast_fusion
  7.9 0.7 convolution_compare_fusion
  8.6 1.6 broadcast_select_fusion
  10.2 0.0 all-gather.3.cloned.1.call-update
  10.2 0.0 reduce-scatter.3.cloned.1.call-start
  10.3 0.9 copy.9
  11.2 0.1 reshape.60
  11.3 7.2 %all_to_all.15 = bf16[4,2,2048]{2,1,0:T(2,128)(2,1)S(1)} all-to-all(bf16[4,2,2048]{2,1,0:T(2,128)(2,1)S(1)} %reshape.60), channel_id=1, replica_groups=mesh['prow'=8,'pcol'=4] {'pcol'}, dimensions={0} | all-to-all | bytes 65536 | tf_op jit(solution)/shard_map/all_to_all | solution.py:49
  18.5 0.1 reshape.61
  18.7 32.7 %all-gather.3.cloned.1.call-done = bf16[2,128,2048]{2,1,0:T(8,128)(2,1)} async-done(((bf16[2,16,2048]{2,1,0:T(8,128)(2,1)}), bf16[2,128,2048]{2,1,0:T(8,128)(2,1)}) %all-gather.3.cloned.1.call-update) | async-done | bytes 1048592 | tf_op jit(solution)/shard_map/all_gather | solution.py:51
  51.4 0.0 copy-start
  51.4 1.4 fusion.6
  52.8 1.3 fusion.5
  54.1 0.0 copy-done
  54.1 0.3 fusion.1
  54.4 0.0 copy-start.2
  54.4 0.3 fusion
  54.7 1.0 pad_maximum_fusion.1
  55.7 0.0 reduce-scatter.3.cloned.1.call-update
  55.8 0.0 reduce-scatter.5.cloned.1.call-start
  55.9 0.0 copy-done.2
  55.9 9.4 %all_gather.10 = bf16[2,64,2048]{2,1,0:T(8,128)(2,1)S(1)} all-gather(bf16[2,16,2048]{2,1,0:T(8,128)(2,1)S(1)} %copy-done.2), channel_id=1, replica_groups=mesh['prow'=8,'pcol'=4] {'pcol'}, dimensions={1}, use_global_device_ids=true | all-gather | bytes 655360 | tf_op jit(solution)/shard_map/all_gather | solution.py:46
  65.2 0.4 fusion.7
  65.6 15.4 %reduce-scatter.3.cloned.1.call-done = f32[2,64,512]{2,1,0:T(8,128)} async-done(((f32[2,64,2048]{2,1,0:T(8,128)}), f32[2,64,512]{2,1,0:T(8,128)}) %reduce-scatter.3.cloned.1.call-update) | async-done | bytes 262160 | tf_op jit(solution)/shard_map/reduce_scatter | solution.py:56
  81.0 1.6 fusion.27
  82.6 0.3 fusion.9
  82.9 0.3 fusion.10
  83.3 0.3 fusion.3
  83.6 0.3 fusion.2
  83.9 1.5 pad_maximum_fusion
  85.4 0.0 copy-start.1
  85.4 0.0 reduce-scatter.5.cloned.1.call-update
  85.4 0.0 all-gather.5.cloned.1.call-start
  85.5 67.0 %reduce-scatter.5.cloned.1.call-done = f32[2,64,512]{2,1,0:T(8,128)} async-done(((f32[2,512,512]{2,1,0:T(8,128)}), f32[2,64,512]{2,1,0:T(8,128)}) %reduce-scatter.5.cloned.1.call-update) | async-done | bytes 262160 | tf_op jit(solution)/shard_map/reduce_scatter | solution.py:68
  152.5 0.0 all-gather.5.cloned.1.call-update
  152.5 49.8 %all-gather.5.cloned.1.call-done = f32[2,512,512]{2,1,0:T(8,128)} async-done(((f32[2,64,512]{2,1,0:T(8,128)}), f32[2,512,512]{2,1,0:T(8,128)}) %all-gather.5.cloned.1.call-update) | async-done | bytes 2097168 | tf_op jit(solution)/shard_map/all_gather | solution.py:71
  202.3 0.0 copy-done.1
  202.3 3.4 %add.76 = f32[2,512,512]{2,1,0:T(8,128)} add(f32[2,512,512]{2,1,0:T(8,128)S(1)} %copy-done.1, f32[2,512,512]{2,1,0:T(8,128)} %all-gather.5.cloned.1.call-done) | non-fusion elementwise | flops 524288 | bytes 6291456 | tf_op jit(solution)/shard_map/add | solution.py:72
  (7 shorter events, 0.1 us)
Async XLA Ops:
  7.2 44.2 %all-gather.3.cloned.1.call-start = ((), (), s32[]{:S(2)}) async-start(), calls=%async_computation.3 | async-start | bytes 1179648 | tf_op jit(solution)/shard_map/all_gather | solution.py:51
  10.2 70.7 %reduce-scatter.3.cloned.1.call-start = ((), (), s32[]{:S(2)}) async-start(), calls=%async_computation.4 | async-start | bytes 1310720 | tf_op jit(solution)/shard_map/reduce_scatter | solution.py:56
  51.4 2.7 %copy-start = (bf16[2,128,2048]{2,1,0:T(8,128)(2,1)S(1)}, bf16[2,128,2048]{2,1,0:T(8,128)(2,1)}, u32[]{:S(2)}) copy-start(bf16[2,128,2048]{2,1,0:T(8,128)(2,1)} %all-gather.3.cloned.1.call-done) | copy-start | bytes 3145732
  54.4 1.5 copy-start.2
  55.8 96.8 %reduce-scatter.5.cloned.1.call-start = ((), (), s32[]{:S(2)}) async-start(), calls=%async_computation.5 | async-start | bytes 2359296 | tf_op jit(solution)/shard_map/reduce_scatter | solution.py:68
  85.4 116.9 %copy-start.1 = (f32[2,512,512]{2,1,0:T(8,128)S(1)}, f32[2,512,512]{2,1,0:T(8,128)}, u32[]{:S(2)}) copy-start(f32[2,512,512]{2,1,0:T(8,128)} %param.7) | copy-start | bytes 6291460
  85.4 116.9 %all-gather.5.cloned.1.call-start = ((), (), s32[]{:S(2)}) async-start(), calls=%async_computation.6 | async-start | bytes 2359296 | tf_op jit(solution)/shard_map/all_gather | solution.py:71
Sparse Core Ops, SparseCore 0:
  10.7 40.6 all-gather.2
  55.9 25.0 reduce-scatter.2
  85.6 66.8 reduce-scatter.4
  154.5 47.7 all-gather.4
where the time goes:
time: 215 us; the launch traced here: 212 us
  waiting for transfers between devices  165 us (77%)
  blocking collectives  16.6 us (8%)
  between operations  13.9 us (6%)
  other arithmetic  9.83 us (5%)
  matrix products  5.66 us (3%)
    reduce_scatter x1, waiting for transfers between devices, local(): lax.psum_scatter(jnp.stack([diag_real, diag_imag]), 'prow', scatter_dimen...  67 us
    all_gather x1, waiting for transfers between devices, local(): correction = lax.all_gather(shares, 'prow', axis=1, tiled=True)  49.8 us
    all_gather x1, waiting for transfers between devices, local(): panel_piece = lax.all_gather(masked, 'prow', axis=1, tiled=True)  32.7 us
    reduce_scatter x1, waiting for transfers between devices, local(): summed = lax.psum_scatter(stacked, 'pcol', scatter_dimension=2, tiled=True)  15.4 us
    all_gather x1, blocking collectives, local(): row_panel = lax.all_gather(masked, 'pcol', axis=1, tiled=True)  9.36 us
    all_to_all x1, blocking collectives, local(): lax.all_to_all(split_cols, 'pcol', split_axis=2, concat_axis=1, tiled=True)  7.22 us
  transfers between devices with their start and end apart: 4, of which 4 were waited for; matrix products, arithmetic and copies ran while one was open for 1% of the time, Pallas kernels for 0%

commit v1 on v0

--- a/solution.py
+++ b/solution.py
@@ -1,9 +1,262 @@
+import functools
+
 import jax
 import jax.numpy as jnp
 from jax import lax
+from jax.experimental import pallas as pl
+from jax.experimental.pallas import tpu as pltpu
 from jax.sharding import PartitionSpec as P
 
 WIDTH = 512
+VMEM_BUDGET = 48 * 2**20
+MESH = pl.DeviceIdType.MESH
+
+
+def row_of(position, half):
+    upper = position // half
+    level = position + upper * (2 * half - 1 - 2 * position)
+    return 2 * level + upper
+
+
+def position_of(row, half):
+    level, upper = row // 2, row % 2
+    return level + upper * (2 * half - 1 - 2 * level)
+
+
+def gather_kernel(
+    ring, pattern, inverse, panel, diag, off_out, diag_out,
+    g, m, masked, coupled, pan, dg,
+    load_sem, ring_send, ring_recv, pan_send, pan_recv,
+    core_send, core_recv, side_send, side_recv, pass_send, pass_recv,
+):
+    half = ring // 2
+    row, col = lax.axis_index("prow"), lax.axis_index("pcol")
+    place = position_of(row, half)
+    rows, part = inverse.shape[1], inverse.shape[2]
+    fine, width = panel.shape[1], diag.shape[2]
+    core_mate = col + 1 - 2 * (col % 2)
+    side_mate = lax.rem(col + 2, 4)
+    far_mate = lax.rem(core_mate + 2, 4)
+    forward = row_of(lax.rem(place + 1, ring), half)
+    backward = row_of(lax.rem(place + ring - 1, ring), half)
+    targets = ((forward, col), (backward, col))
+
+    def block_row(offset):
+        return row_of(lax.rem(place + ring + offset, ring), half)
+
+    def g_part(of_row, of_col):
+        return g.at[
+            :,
+            pl.ds(pl.multiple_of(of_row * rows, rows), rows),
+            pl.ds(pl.multiple_of(of_col * part, part), part),
+        ]
+
+    def m_part(of_row, of_col, first=0, count=2):
+        start = pl.multiple_of(of_row * rows + of_col * fine, fine)
+        return m.at[pl.ds(first, count), pl.ds(start, fine), :]
+
+    def own_columns(of_col):
+        return pan.at[:, :, pl.ds(pl.multiple_of(of_col * width, width), width)]
+
+    load_panel = pltpu.make_async_copy(panel, pan, load_sem.at[0])
+    load_g = pltpu.make_async_copy(inverse, g_part(row, col), load_sem.at[1])
+    load_diag = pltpu.make_async_copy(diag, dg, load_sem.at[2])
+    load_panel.start()
+    load_g.start()
+
+    barrier = pltpu.get_barrier_semaphore()
+    partners = targets + ((row, core_mate), (row, side_mate), (row, far_mate))
+    for partner in partners:
+        pl.semaphore_signal(barrier, inc=1, device_id=partner, device_id_type=MESH)
+    pl.semaphore_wait(barrier, len(partners))
+    load_panel.wait()
+    load_g.wait()
+
+    started = []
+
+    def send(src, dst, send_sem, recv_sem, target):
+        copy = pltpu.make_async_remote_copy(
+            src_ref=src, dst_ref=dst, send_sem=send_sem, recv_sem=recv_sem,
+            device_id=target, device_id_type=MESH,
+        )
+        copy.start()
+        started.append(copy)
+
+    mates = (core_mate, side_mate, far_mate)
+    sources = (col,) + mates
+
+    def piece(offset, chunk):
+        of_row = block_row(offset)
+        if chunk == 0:
+            return g_part(of_row, col)
+        if chunk == 5:
+            return m_part(of_row, side_mate, 0, 1)
+        if chunk == 6:
+            return m_part(of_row, side_mate, 1, 1)
+        return m_part(of_row, sources[chunk - 1])
+
+    full = (0, 1, 2, 3, 4)
+    split = ((0, 1, 5), (2, 4, 6))
+
+    def carried(d, hop):
+        return full if hop < half else split[d]
+
+    def hop_offset(d, hop):
+        return -hop if d == 0 else hop
+
+    def wait_recv(ref, sem):
+        pltpu.make_async_copy(ref, ref, sem).wait()
+
+    def ring_send_piece(d, hop, chunk, src=None):
+        offset = hop_offset(d, hop - 1)
+        ref = piece(offset, chunk)
+        send(
+            ref if src is None else src, ref,
+            ring_send.at[d, hop - 1, chunk], ring_recv.at[d, hop - 1, chunk],
+            targets[d],
+        )
+
+    def share_g(index, offset):
+        ref = g_part(block_row(offset), col)
+        send(ref, ref, core_send.at[index], core_recv.at[index], (row, core_mate))
+        send(ref, ref, side_send.at[index], side_recv.at[index], (row, side_mate))
+
+    def pass_g(index, offset):
+        ref = g_part(block_row(offset), side_mate)
+        wait_recv(ref, side_recv.at[index])
+        send(ref, ref, pass_send.at[index], pass_recv.at[index], (row, core_mate))
+
+    for d in (0, 1):
+        ring_send_piece(d, 1, 0)
+    for index in (1, 2, 0):
+        send(
+            own_columns(mates[index]), m_part(row, col),
+            pan_send.at[index], pan_recv.at[index], (row, mates[index]),
+        )
+    for d in (0, 1):
+        ring_send_piece(d, 1, 1, own_columns(col))
+    share_g(0, 0)
+    keep_own = pltpu.make_async_copy(own_columns(col), m_part(row, col), load_sem.at[3])
+    keep_own.start()
+    load_diag.start()
+    for index in range(3):
+        wait_recv(m_part(row, mates[index]), pan_recv.at[index])
+        for d in (0, 1):
+            ring_send_piece(d, 1, index + 2)
+    pass_g(0, 0)
+    blocks = [(0, 0)]
+    for hop in range(1, half + 1):
+        fresh = []
+        order = full + (5, 6)
+        for chunk in order:
+            for d in (0, 1):
+                if chunk not in carried(d, hop):
+                    continue
+                offset = hop_offset(d, hop)
+                wait_recv(piece(offset, chunk), ring_recv.at[d, hop - 1, chunk])
+                if hop + 1 < half:
+                    ring_send_piece(d, hop + 1, chunk)
+                elif hop + 1 == half:
+                    if chunk in split[d]:
+                        ring_send_piece(d, half, chunk)
+                    elif chunk == 3:
+                        ring_send_piece(d, half, 5 + d)
+                if chunk == 0:
+                    index = len(blocks)
+                    blocks.append((index, offset))
+                    fresh.append((index, offset))
+                    share_g(index, offset)
+            if chunk == 3 and hop < half:
+                for index, offset in fresh:
+                    pass_g(index, offset)
+                fresh = []
+        for index, offset in fresh:
+            pass_g(index, offset)
+    for index, offset in blocks:
+        wait_recv(g_part(block_row(offset), core_mate), core_recv.at[index])
+        wait_recv(g_part(block_row(offset), far_mate), pass_recv.at[index])
+    keep_own.wait()
+
+    super_index = col * width // WIDTH
+    order_rows = g.shape[1]
+    for block in range(order_rows // WIDTH):
+        keep = pattern[block, super_index] > 0
+        span = slice(block * WIDTH, (block + 1) * WIDTH)
+        masked[:, span, :] = jnp.where(keep, m[:, span, :], jnp.zeros_like(m[:, span, :]))
+
+    def dot(a, b, contract):
+        return lax.dot_general(
+            a, b, (((contract,), (0,)), ((), ())), preferred_element_type=jnp.float32
+        )
+
+    step = min(256, width)
+    for start in range(0, width, step):
+        cols = slice(start, start + step)
+        real = dot(g[0], masked[0, :, cols], 1) - dot(g[1], masked[1, :, cols], 1)
+        imag = dot(g[0], masked[1, :, cols], 1) + dot(g[1], masked[0, :, cols], 1)
+        for block in range(order_rows // WIDTH):
+            keep = (pattern[block, super_index] > 0).astype(jnp.float32)
+            span = slice(block * WIDTH, (block + 1) * WIDTH)
+            coupled[0, span, cols] = (real[span] * keep).astype(jnp.bfloat16)
+            coupled[1, span, cols] = (imag[span] * keep).astype(jnp.bfloat16)
+    off_out[...] = -coupled[:, pl.ds(pl.multiple_of(row * rows, rows), rows), :]
+    load_diag.wait()
+    for start in range(0, width, step):
+        cols = slice(start, start + step)
+        diag_out[0, :, cols] = dg[0, :, cols] + (
+            dot(masked[0], coupled[0, :, cols], 0) - dot(masked[1], coupled[1, :, cols], 0)
+        )
+        diag_out[1, :, cols] = dg[1, :, cols] + (
+            dot(masked[0], coupled[1, :, cols], 0) + dot(masked[1], coupled[0, :, cols], 0)
+        )
+    for copy in started:
+        copy.wait_send()
+
+
+def gathered(inverse_block, panel, pattern, diag_inverse):
+    ring = lax.axis_size("prow")
+    half = ring // 2
+    rows = inverse_block.shape[1]
+    order, width = rows * ring, diag_inverse.shape[2]
+    dma = pltpu.SemaphoreType.DMA
+    anywhere = pl.BlockSpec(memory_space=pl.ANY)
+    whole = pl.BlockSpec(memory_space=pltpu.VMEM)
+    return pl.pallas_call(
+        functools.partial(gather_kernel, ring),
+        out_shape=(
+            jax.ShapeDtypeStruct((2, rows, width), jnp.bfloat16),
+            jax.ShapeDtypeStruct(diag_inverse.shape, jnp.float32),
+        ),
+        in_specs=[pl.BlockSpec(memory_space=pltpu.SMEM), anywhere, anywhere, anywhere],
+        out_specs=(whole, whole),
+        scratch_shapes=[
+            pltpu.VMEM((2, order, order), jnp.bfloat16),
+            pltpu.VMEM((2, order, width), jnp.bfloat16),
+            pltpu.VMEM((2, order, width), jnp.bfloat16),
+            pltpu.VMEM((2, order, width), jnp.bfloat16),
+            pltpu.VMEM(panel.shape, jnp.bfloat16),
+            pltpu.VMEM(diag_inverse.shape, jnp.float32),
+            dma((4,)),
+            dma((2, half, 7)), dma((2, half, 7)),
+            dma((3,)), dma((3,)),
+            dma((ring,)), dma((ring,)),
+            dma((ring,)), dma((ring,)),
+            dma((ring,)), dma((ring,)),
+        ],
+        compiler_params=pltpu.CompilerParams(
+            collective_id=0, has_side_effects=True, vmem_limit_bytes=VMEM_BUDGET
+        ),
+    )(pattern, inverse_block, panel, diag_inverse)
+
+
+def fits(ring, col_count, inverse_block, panel, diag_inverse):
+    order, width = inverse_block.shape[1] * ring, diag_inverse.shape[2]
+    held = 4 * order * order + 8 * order * width + 16 * diag_inverse.shape[1] * width
+    return (
+        ring % 2 == 0 and ring >= 4 and col_count == 4 and width == WIDTH
+        and panel.shape[1] % 16 == 0 and inverse_block.shape[2] % 128 == 0
+        and order % WIDTH == 0 and held <= VMEM_BUDGET * 2 // 3
+    )
 
 
 def complex_product(left_real, left_imag, right_real, right_imag, contract):
@@ -36,6 +289,8 @@
     block_span = inverse_block.shape[2]
     fine_rows = panel.shape[1]
     columns = panel.shape[2]
+    if fits(lax.axis_size("prow"), lax.axis_size("pcol"), inverse_block, panel, diag_inverse):
+        return gathered(inverse_block, panel, pattern, diag_inverse)
     row_index = lax.axis_index("prow")
     col_index = lax.axis_index("pcol")
     col_count = lax.axis_size("pcol")

time: 215 us -> 34.2 us (0.16); the launches traced: 212 us -> 33.9 us
  waiting for transfers between devices: 165 us -> 0 us
  Pallas kernels: 0 us -> 27.4 us
  blocking collectives: 16.6 us -> 0 us
  between operations: 13.9 us -> 0.65 us
  other arithmetic: 9.83 us -> 0 us
  matrix products: 5.66 us -> 0 us
  local copies, waits for them, and re-layouts: 1.14 us -> 5.88 us
    all_gather x2 -> x0, waiting for transfers between devices: 82.5 us -> none  [the longest x1 49.8 us: local(): correction = lax.all_gather(shares, 'prow', axis=1, tiled=True)]
    reduce_scatter x2 -> x0, waiting for transfers between devices: 82.4 us -> none  [the longest x1 67 us: local(): lax.psum_scatter(jnp.stack([diag_real, diag_imag]), 'prow', scatter_dimen...]
    pallas_call x0 -> x1, Pallas kernels: none -> 27.4 us  [gathered(): pl.pallas_call(functools.partial(gather_kernel, ring), out_shape=(jax.Sha...]
    all_gather x1 -> x0, blocking collectives: 9.36 us -> none  [local(): row_panel = lax.all_gather(masked, 'pcol', axis=1, tiled=True)]
    all_to_all x1 -> x0, blocking collectives: 7.22 us -> none  [local(): lax.all_to_all(split_cols, 'pcol', split_axis=2, concat_axis=1, tiled=True)]
    dot_general x10 -> x0, matrix products: 5.66 us -> none  [the longest x2 1.72 us: complex_product(): lax.dot_general(left_real, right_imag, dims, preferred_element_type=jnp.f...]
    unnamed x9 -> x10, local copies, waits for them, and re-layouts: 1.12 us -> 5.88 us
    add x1 -> x0, other arithmetic: 3.39 us -> none  [local(): return (offdiag, diag_inverse + correction)]
  transfers between devices with their start and end apart: 4 -> 0, of which waited for: 4 -> 0; matrix products, arithmetic and copies ran while one was open for 1% -> 0% of each run, Pallas kernels for 0% -> 0%
where the time goes in v1:
time: 34.2 us; the launch traced here: 33.9 us
  Pallas kernels  27.4 us (80%)
  local copies, waits for them, and re-layouts  5.88 us (17%)
  between operations  0.65 us (2%)
    pallas_call x1, Pallas kernels, gathered(): pl.pallas_call(functools.partial(gather_kernel, ring), out_shape=(jax.Sha...  27.4 us
    unnamed x10, local copies, waits for them, and re-layouts  5.88 us

profile of v1, /device:TPU:1, one launch (start us, length us, event | category | flops | bytes accessed | tf_op | source)
XLA Modules:
  0.0 33.9 jit_solution(2507017850993475792)
XLA Ops:
  0.6 0.0 copy-start
  0.6 1.6 %copy-done = f32[2,512,512]{2,1,0:T(8,128)S(1)} copy-done((f32[2,512,512]{2,1,0:T(8,128)S(1)}, f32[2,512,512]{2,1,0:T(8,128)}, u32[]{:S(2)}) %copy-start) | copy-done | bytes 2097176
  2.2 0.0 copy-start.1
  2.2 0.9 %copy-done.1 = bf16[2,16,2048]{2,1,0:T(8,128)(2,1)S(1)} copy-done((bf16[2,16,2048]{2,1,0:T(8,128)(2,1)S(1)}, bf16[2,16,2048]{2,1,0:T(8,128)(2,1)}, u32[]{:S(2)}) %copy-start.1) | copy-done | bytes 131096
  3.1 0.0 copy-start.2
  3.1 0.8 %copy-done.2 = bf16[2,64,128]{2,1,0:T(8,128)(2,1)S(1)} copy-done((bf16[2,64,128]{2,1,0:T(8,128)(2,1)S(1)}, bf16[2,64,128]{2,1,0:T(8,128)(2,1)}, u32[]{:S(2)}) %copy-start.2) | copy-done | bytes 32792
  3.9 0.0 copy-start.3
  3.9 0.7 %copy-done.3 = s32[1,4]{1,0:T(1,128)S(1)} copy-done((s32[1,4]{1,0:T(1,128)S(1)}, s32[1,4]{1,0:T(1,128)}, u32[]{:S(2)}) %copy-start.3) | copy-done | bytes 40
  4.5 27.4 %shard_map.59 = (bf16[2,64,512]{2,1,0:T(8,128)(2,1)S(1)}, f32[2,512,512]{2,1,0:T(8,128)S(1)}) custom-call(s32[1,4]{1,0:T(1,128)S(1)} %copy-done.3, bf16[2,64,128]{2,1,0:T(8,128)(2,1)S(1)} %copy-done.2, bf16[2,16,2048]{2,1,0:T(8,128)(2,1)S(1)} %copy-done.1, f32[2,512,512]{2,1,0:T(8,128)S(1)} %copy-done), custom_call_target="tpu_custom_call" | custom-call | tf_op jit(solution)/shard_map/pallas_call | solution.py:224
  32.0 0.7 %copy.8 = bf16[2,64,512]{2,1,0:T(8,128)(2,1)} copy(bf16[2,64,512]{2,1,0:T(8,128)(2,1)S(1)} %get-tuple-element.4) | data formatting | bytes 262144
  32.6 1.3 %copy.9 = f32[2,512,512]{2,1,0:T(8,128)} copy(f32[2,512,512]{2,1,0:T(8,128)S(1)} %get-tuple-element.5) | data formatting | bytes 4194304
Async XLA Ops:
  0.6 1.6 %copy-start = (f32[2,512,512]{2,1,0:T(8,128)S(1)}, f32[2,512,512]{2,1,0:T(8,128)}, u32[]{:S(2)}) copy-start(f32[2,512,512]{2,1,0:T(8,128)} %diag.1) | copy-start | bytes 6291460
  2.2 0.9 %copy-start.1 = (bf16[2,16,2048]{2,1,0:T(8,128)(2,1)S(1)}, bf16[2,16,2048]{2,1,0:T(8,128)(2,1)}, u32[]{:S(2)}) copy-start(bf16[2,16,2048]{2,1,0:T(8,128)(2,1)} %panel.1) | copy-start | bytes 393220
  3.1 0.8 %copy-start.2 = (bf16[2,64,128]{2,1,0:T(8,128)(2,1)S(1)}, bf16[2,64,128]{2,1,0:T(8,128)(2,1)}, u32[]{:S(2)}) copy-start(bf16[2,64,128]{2,1,0:T(8,128)(2,1)} %inverse.1) | copy-start | bytes 98308
  3.9 0.7 %copy-start.3 = (s32[1,4]{1,0:T(1,128)S(1)}, s32[1,4]{1,0:T(1,128)}, u32[]{:S(2)}) copy-start(s32[1,4]{1,0:T(1,128)} %pattern.1) | copy-start | bytes 52

commit v2 on v0

--- a/solution.py
+++ b/solution.py
@@ -1,9 +1,367 @@
+import functools
+import heapq
+
 import jax
 import jax.numpy as jnp
 from jax import lax
+from jax.experimental import pallas as pl
+from jax.experimental.pallas import tpu as pltpu
 from jax.sharding import PartitionSpec as P
 
 WIDTH = 512
+VMEM_BUDGET = 48 * 2**20
+MESH = pl.DeviceIdType.MESH
+
+
+def row_of(position, half):
+    upper = position // half
+    level = position + upper * (2 * half - 1 - 2 * position)
+    return 2 * level + upper
+
+
+def position_of(row, half):
+    level, upper = row // 2, row % 2
+    return level + upper * (2 * half - 1 - 2 * level)
+
+
+def schedule(half, full, split, piece_time, link_delay, core_delay):
+    free = {"ring0": 0.0, "ring1": 0.0, "side": 0.0, "core": 0.0}
+    heap, order, serial = [], [], [0]
+
+    def post(now, link, key, size=1.0):
+        span = size * (piece_time if link != "core" else piece_time / 8)
+        begin = max(now, free[link])
+        free[link] = begin + span
+        delay = core_delay if link == "core" else link_delay
+        serial[0] += 1
+        heapq.heappush(heap, (begin + span + delay, serial[0], key))
+
+    def ring(now, d, hop, chunk):
+        post(now, "ring%d" % d, ("ring", d, hop, chunk), 0.5 if chunk > 4 else 1.0)
+
+    def share(now, index):
+        post(now, "core", ("core", index))
+        post(now, "side", ("side", index))
+
+    for d in (0, 1):
+        ring(0.0, d, 1, 0)
+    post(0.0, "core", ("pan", 0))
+    for index in (1, 2):
+        post(0.0, "side", ("pan", index))
+    for d in (0, 1):
+        ring(0.0, d, 1, 1)
+    share(0.0, (0, 0))
+    while heap:
+        now, _, key = heapq.heappop(heap)
+        order.append(key)
+        if key[0] == "pan":
+            for d in (0, 1):
+                ring(now, d, 1, key[1] + 2)
+        elif key[0] == "side":
+            post(now, "core", ("pass", key[1]))
+        elif key[0] == "ring":
+            _, d, hop, chunk = key
+            for onward in carried_on(half, full, split, d, hop, chunk):
+                ring(now, d, hop + 1, onward)
+            if chunk == 0:
+                share(now, (d, hop))
+    return order
+
+
+def carried_on(half, full, split, d, hop, chunk):
+    if hop + 1 < half:
+        return (chunk,)
+    if hop + 1 > half:
+        return ()
+    if chunk in split[d]:
+        return (chunk,)
+    return (5 + d,) if chunk == 3 else ()
+
+
+FULL = (0, 1, 2, 3, 4)
+SPLIT = ((0, 1, 5), (2, 4, 6))
+
+
+def gather_kernel(
+    ring, pattern_hbm, inverse, panel, diag, masked, coupled, held,
+    pattern, g, m, pan, acc, tail,
+    load_sem, ring_send, ring_recv, pan_send, pan_recv,
+    core_send, core_recv, side_send, side_recv, pass_send, pass_recv,
+):
+    half = ring // 2
+    row, col = lax.axis_index("prow"), lax.axis_index("pcol")
+    place = position_of(row, half)
+    rows, part = inverse.shape[1], inverse.shape[2]
+    fine, width = panel.shape[1], masked.shape[2]
+    order_rows = g.shape[1]
+    core_mate = col + 1 - 2 * (col % 2)
+    side_mate = lax.rem(col + 2, 4)
+    far_mate = lax.rem(core_mate + 2, 4)
+    forward = row_of(lax.rem(place + 1, ring), half)
+    backward = row_of(lax.rem(place + ring - 1, ring), half)
+    targets = ((forward, col), (backward, col))
+    mates = (core_mate, side_mate, far_mate)
+    sources = (col,) + mates
+
+    def block_row(offset):
+        return row_of(lax.rem(place + ring + offset, ring), half)
+
+    def g_part(of_row, of_col):
+        return g.at[
+            :,
+            pl.ds(pl.multiple_of(of_row * rows, rows), rows),
+            pl.ds(pl.multiple_of(of_col * part, part), part),
+        ]
+
+    def m_part(of_row, of_col, first=0, count=2):
+        start = pl.multiple_of(of_row * rows + of_col * fine, fine)
+        return m.at[pl.ds(first, count), pl.ds(start, fine), :]
+
+    def own_columns(of_col):
+        return pan.at[:, :, pl.ds(pl.multiple_of(of_col * width, width), width)]
+
+    load_panel = pltpu.make_async_copy(panel, pan, load_sem.at[0])
+    load_g = pltpu.make_async_copy(inverse, g_part(row, col), load_sem.at[1])
+    load_pattern = pltpu.make_async_copy(pattern_hbm, pattern, load_sem.at[2])
+    load_g.start()
+    load_panel.start()
+    load_pattern.start()
+
+    barrier = pltpu.get_barrier_semaphore()
+    partners = targets + tuple((row, mate) for mate in mates)
+    for partner in partners:
+        pl.semaphore_signal(barrier, inc=1, device_id=partner, device_id_type=MESH)
+    pl.semaphore_wait(barrier, len(partners))
+
+    started = []
+
+    def send(src, dst, send_sem, recv_sem, target):
+        copy = pltpu.make_async_remote_copy(
+            src_ref=src, dst_ref=dst, send_sem=send_sem, recv_sem=recv_sem,
+            device_id=target, device_id_type=MESH,
+        )
+        copy.start()
+        started.append(copy)
+
+    def piece(offset, chunk):
+        of_row = block_row(offset)
+        if chunk == 0:
+            return g_part(of_row, col)
+        if chunk > 4:
+            return m_part(of_row, side_mate, chunk - 5, 1)
+        return m_part(of_row, sources[chunk - 1])
+
+    def offset_of(key):
+        return -key[1] if key[0] == 0 else key[1]
+
+    def slot(key):
+        return key[0] * half + key[1]
+
+    def wait_recv(ref, sem):
+        pltpu.make_async_copy(ref, ref, sem).wait()
+
+    def ring_on(d, hop, chunk, src=None):
+        ref = piece(offset_of((d, hop - 1)), chunk)
+        send(
+            ref if src is None else src, ref,
+            ring_send.at[d, hop - 1, chunk], ring_recv.at[d, hop - 1, chunk], targets[d],
+        )
+
+    def share_g(key):
+        ref, at = g_part(block_row(offset_of(key)), col), slot(key)
+        send(ref, ref, core_send.at[at], core_recv.at[at], (row, core_mate))
+        send(ref, ref, side_send.at[at], side_recv.at[at], (row, side_mate))
+
+    def handle(key):
+        if key[0] == "pan":
+            wait_recv(m_part(row, mates[key[1]]), pan_recv.at[key[1]])
+            for d in (0, 1):
+                ring_on(d, 1, key[1] + 2)
+        elif key[0] == "side":
+            ref, at = g_part(block_row(offset_of(key[1])), side_mate), slot(key[1])
+            wait_recv(ref, side_recv.at[at])
+            send(ref, ref, pass_send.at[at], pass_recv.at[at], (row, core_mate))
+        elif key[0] == "core":
+            wait_recv(g_part(block_row(offset_of(key[1])), core_mate), core_recv.at[slot(key[1])])
+        elif key[0] == "pass":
+            wait_recv(g_part(block_row(offset_of(key[1])), far_mate), pass_recv.at[slot(key[1])])
+        else:
+            _, d, hop, chunk = key
+            wait_recv(piece(offset_of((d, hop)), chunk), ring_recv.at[d, hop - 1, chunk])
+            for onward in carried_on(half, FULL, SPLIT, d, hop, chunk):
+                ring_on(d, hop + 1, onward)
+            if chunk == 0:
+                share_g((d, hop))
+
+    load_g.wait()
+    for d in (0, 1):
+        ring_on(d, 1, 0)
+    load_panel.wait()
+    for index in (1, 2, 0):
+        send(
+            own_columns(mates[index]), m_part(row, col),
+            pan_send.at[index], pan_recv.at[index], (row, mates[index]),
+        )
+    for d in (0, 1):
+        ring_on(d, 1, 1, own_columns(col))
+    share_g((0, 0))
+    keep_own = pltpu.make_async_copy(own_columns(col), m_part(row, col), load_sem.at[3])
+    keep_own.start()
+    load_diag = pltpu.make_async_copy(diag, held, load_sem.at[4])
+    load_diag.start()
+
+    keys = schedule(half, FULL, SPLIT, 0.78, 1.65, 0.9)
+    last = [k for k in keys if k[0] == "ring" and k[2] == half and k[3] > 0]
+    inert = [k for k in keys if k[0] in ("core", "pass")]
+    for key in keys:
+        if key not in last and key not in inert:
+            handle(key)
+    keep_own.wait()
+    load_diag.wait()
+    load_pattern.wait()
+
+    super_index = col * width // WIDTH
+
+    def rows_of(of_row):
+        return pl.ds(pl.multiple_of(of_row * rows, rows), rows)
+
+    def masked_rows(of_row):
+        keep = pattern[of_row * rows // WIDTH, super_index] > 0
+        values = m[:, rows_of(of_row), :]
+        return jnp.where(keep, values, jnp.zeros_like(values))
+
+    far_row = block_row(half)
+    for offset in range(1 - half, half):
+        of_row = block_row(offset)
+        masked[:, rows_of(of_row), :] = masked_rows(of_row)
+    masked[:, rows_of(far_row), :] = jnp.zeros((2, rows, width), masked.dtype)
+    for key in inert:
+        handle(key)
+
+    step = min(256, width)
+    for start in range(0, width, step):
+        cols = slice(start, start + step)
+        acc[0, :, cols] = dot(g[0], masked[0, :, cols], 1) - dot(g[1], masked[1, :, cols], 1)
+        acc[1, :, cols] = dot(g[0], masked[1, :, cols], 1) + dot(g[1], masked[0, :, cols], 1)
+
+    for key in last:
+        handle(key)
+    span = tail.shape[1]
+    tail[...] = jnp.zeros_like(tail)
+    far_values = masked_rows(far_row)
+    masked[:, rows_of(far_row), :] = far_values
+    tail[:, pl.ds(pl.multiple_of(lax.rem(far_row * rows, span), rows), rows), :] = far_values
+    lanes = pl.ds(pl.multiple_of(far_row * rows // span * span, span), span)
+    for start in range(0, width, step):
+        cols = slice(start, start + step)
+        real = acc[0, :, cols] + (
+            dot(g[0, :, lanes], tail[0, :, cols], 1) - dot(g[1, :, lanes], tail[1, :, cols], 1)
+        )
+        imag = acc[1, :, cols] + (
+            dot(g[0, :, lanes], tail[1, :, cols], 1) + dot(g[1, :, lanes], tail[0, :, cols], 1)
+        )
+        for block in range(order_rows // WIDTH):
+            keep = (pattern[block, super_index] > 0).astype(jnp.float32)
+            band = slice(block * WIDTH, (block + 1) * WIDTH)
+            coupled[0, band, cols] = (real[band] * keep).astype(jnp.bfloat16)
+            coupled[1, band, cols] = (imag[band] * keep).astype(jnp.bfloat16)
+    for copy in started:
+        copy.wait_send()
+
+
+def dot(a, b, contract):
+    return lax.dot_general(
+        a, b, (((contract,), (0,)), ((), ())), preferred_element_type=jnp.float32
+    )
+
+
+def correct_kernel(masked, coupled, held, off_out, diag_out, off, total, save_sem):
+    rows, height = off.shape[1], total.shape[1]
+    row = lax.axis_index("prow")
+    off[...] = -coupled[:, pl.ds(pl.multiple_of(row * rows, rows), rows), :]
+    saves = [pltpu.make_async_copy(off, off_out, save_sem.at[0])]
+    saves[0].start()
+    step = min(256, height)
+    for start in range(0, height, step):
+        span = slice(start, start + step)
+        for which in (0, 1):
+            first = dot(masked[0, :, span], coupled[which], 0)
+            second = dot(masked[1, :, span], coupled[1 - which], 0)
+            total[which, span, :] = held[which, span, :] + (
+                first - second if which == 0 else first + second
+            )
+            save = pltpu.make_async_copy(
+                total.at[which, span, :], diag_out.at[which, span, :], save_sem.at[len(saves)]
+            )
+            save.start()
+            saves.append(save)
+    for save in saves:
+        save.wait()
+
+
+def in_hbm(array):
+    return pltpu.with_memory_space_constraint(array, pltpu.HBM)
+
+
+def gathered(inverse_block, panel, pattern, diag_inverse):
+    ring = lax.axis_size("prow")
+    half = ring // 2
+    rows = inverse_block.shape[1]
+    order, width, height = rows * ring, diag_inverse.shape[2], diag_inverse.shape[1]
+    dma = pltpu.SemaphoreType.DMA
+    anywhere = pl.BlockSpec(memory_space=pl.ANY)
+    whole = pl.BlockSpec(memory_space=pltpu.VMEM)
+    tall = jax.ShapeDtypeStruct((2, order, width), jnp.bfloat16)
+    masked, coupled, held = pl.pallas_call(
+        functools.partial(gather_kernel, ring),
+        out_shape=(tall, tall, jax.ShapeDtypeStruct(diag_inverse.shape, jnp.float32)),
+        in_specs=[anywhere] * 4,
+        out_specs=(whole,) * 3,
+        scratch_shapes=[
+            pltpu.SMEM(pattern.shape, jnp.int32),
+            pltpu.VMEM((2, order, order), jnp.bfloat16),
+            pltpu.VMEM((2, order, width), jnp.bfloat16),
+            pltpu.VMEM(panel.shape, jnp.bfloat16),
+            pltpu.VMEM((2, order, width), jnp.float32),
+            pltpu.VMEM((2, max(rows, 128), width), jnp.bfloat16),
+            dma((5,)),
+            dma((2, half, 7)), dma((2, half, 7)),
+            dma((3,)), dma((3,)),
+            dma((ring + 1,)), dma((ring + 1,)),
+            dma((ring + 1,)), dma((ring + 1,)),
+            dma((ring + 1,)), dma((ring + 1,)),
+        ],
+        compiler_params=pltpu.CompilerParams(
+            collective_id=0, has_side_effects=True, vmem_limit_bytes=VMEM_BUDGET
+        ),
+    )(in_hbm(pattern), in_hbm(inverse_block), in_hbm(panel), in_hbm(diag_inverse))
+    return pl.pallas_call(
+        correct_kernel,
+        out_shape=(
+            jax.ShapeDtypeStruct((2, rows, width), jnp.bfloat16),
+            jax.ShapeDtypeStruct(diag_inverse.shape, jnp.float32),
+        ),
+        in_specs=[whole] * 3,
+        out_specs=(anywhere, anywhere),
+        scratch_shapes=[
+            pltpu.VMEM((2, rows, width), jnp.bfloat16),
+            pltpu.VMEM(diag_inverse.shape, jnp.float32),
+            dma((2 * pl.cdiv(height, 256) + 1,)),
+        ],
+        compiler_params=pltpu.CompilerParams(vmem_limit_bytes=VMEM_BUDGET),
+    )(masked, coupled, held)
+
+
+def fits(ring, col_count, inverse_block, panel, diag_inverse):
+    rows, width = inverse_block.shape[1], diag_inverse.shape[2]
+    order = rows * ring
+    held = 4 * order * order + 8 * order * width + 16 * diag_inverse.shape[1] * width
+    return (
+        ring % 2 == 0 and ring >= 4 and col_count == 4 and width == WIDTH
+        and panel.shape[1] % 16 == 0 and inverse_block.shape[2] % 128 == 0
+        and order % WIDTH == 0 and max(rows, 128) % rows == 0 and rows % 16 == 0
+        and WIDTH % rows == 0 and held <= VMEM_BUDGET * 2 // 3
+    )
 
 
 def complex_product(left_real, left_imag, right_real, right_imag, contract):
@@ -36,6 +394,8 @@
     block_span = inverse_block.shape[2]
     fine_rows = panel.shape[1]
     columns = panel.shape[2]
+    if fits(lax.axis_size("prow"), lax.axis_size("pcol"), inverse_block, panel, diag_inverse):
+        return gathered(inverse_block, panel, pattern, diag_inverse)
     row_index = lax.axis_index("prow")
     col_index = lax.axis_index("pcol")
     col_count = lax.axis_size("pcol")

time: 215 us -> 27.9 us (0.13); the launches traced: 212 us -> 27.7 us
  waiting for transfers between devices: 165 us -> 0 us
  Pallas kernels: 0 us -> 27.1 us
  blocking collectives: 16.6 us -> 0 us
  between operations: 13.9 us -> 0.64 us
  other arithmetic: 9.83 us -> 0 us
  matrix products: 5.66 us -> 0 us
    all_gather x2 -> x0, waiting for transfers between devices: 82.5 us -> none  [the longest x1 49.8 us: local(): correction = lax.all_gather(shares, 'prow', axis=1, tiled=True)]
    reduce_scatter x2 -> x0, waiting for transfers between devices: 82.4 us -> none  [the longest x1 67 us: local(): lax.psum_scatter(jnp.stack([diag_real, diag_imag]), 'prow', scatter_dimen...]
    pallas_call x0 -> x2, Pallas kernels: none -> 27.1 us  [the longest x1 25 us: gathered(): pl.pallas_call(functools.partial(gather_kernel, ring), out_shape=(tall, t...]
    all_gather x1 -> x0, blocking collectives: 9.36 us -> none  [local(): row_panel = lax.all_gather(masked, 'pcol', axis=1, tiled=True)]
    all_to_all x1 -> x0, blocking collectives: 7.22 us -> none  [local(): lax.all_to_all(split_cols, 'pcol', split_axis=2, concat_axis=1, tiled=True)]
    dot_general x10 -> x0, matrix products: 5.66 us -> none  [the longest x2 1.72 us: complex_product(): lax.dot_general(left_real, right_imag, dims, preferred_element_type=jnp.f...]
    add x1 -> x0, other arithmetic: 3.39 us -> none  [local(): return (offdiag, diag_inverse + correction)]
    another operation x5 -> x0, other arithmetic: 3.22 us -> none  [the longest x1 1.49 us: local(): jnp.stack([diag_real, diag_imag])]
  transfers between devices with their start and end apart: 4 -> 0, of which waited for: 4 -> 0; matrix products, arithmetic and copies ran while one was open for 1% -> 0% of each run, Pallas kernels for 0% -> 0%
where the time goes in v2:
time: 27.9 us; the launch traced here: 27.7 us
  Pallas kernels  27.1 us (97%)
  between operations  0.64 us (2%)
    pallas_call x1, Pallas kernels, gathered(): pl.pallas_call(functools.partial(gather_kernel, ring), out_shape=(tall, t...  25 us
    pallas_call x1, Pallas kernels, gathered(): pl.pallas_call(correct_kernel, out_shape=(jax.ShapeDtypeStruct((2, rows,...  2.13 us

profile of v2, /device:TPU:1, one launch (start us, length us, event | category | flops | bytes accessed | tf_op | source)
XLA Modules:
  0.0 27.7 jit_solution(14979055823720875859)
XLA Ops:
  0.6 25.0 %shard_map.59 = (bf16[2,512,512]{2,1,0:T(8,128)(2,1)S(1)}, bf16[2,512,512]{2,1,0:T(8,128)(2,1)S(1)}, f32[2,512,512]{2,1,0:T(8,128)S(1)}) custom-call(s32[1,4]{1,0:T(1,128)} %pattern_hbm.1, bf16[2,64,128]{2,1,0:T(8,128)(2,1)} %inverse.1, bf16[2,16,2048]{2,1,0:T(8,128)(2,1)} %panel.1, f32[2,512,512]{2,1,0:T(8,128)} %diag.1), custom_call_target="tpu_custom_call" | custom-call | tf_op jit(solution)/shard_map/pallas_call | solution.py:315
  25.6 2.1 %shard_map.60 = (bf16[2,64,512]{2,1,0:T(8,128)(2,1)}, f32[2,512,512]{2,1,0:T(8,128)}) custom-call(bf16[2,512,512]{2,1,0:T(8,128)(2,1)S(1)} %get-tuple-element.5.masked, bf16[2,512,512]{2,1,0:T(8,128)(2,1)S(1)} %get-tuple-element.6.coupled, f32[2,512,512]{2,1,0:T(8,128)S(1)} %get-tuple-element.7.held), custom_call_target="tpu_custom_call" | custom-call | tf_op jit(solution)/shard_map/pallas_call | solution.py:338

commit v3 on v2

--- a/solution.py
+++ b/solution.py
@@ -24,9 +24,9 @@
     return level + upper * (2 * half - 1 - 2 * level)
 
 
-def schedule(half, full, split, piece_time, link_delay, core_delay):
+def schedule(half, piece_time, link_delay, core_delay, backlog):
     free = {"ring0": 0.0, "ring1": 0.0, "side": 0.0, "core": 0.0}
-    heap, order, serial = [], [], [0]
+    heap, order, serial, held = [], [], [0], ([], [])
 
     def post(now, link, key, size=1.0):
         span = size * (piece_time if link != "core" else piece_time / 8)
@@ -38,10 +38,16 @@
 
     def ring(now, d, hop, chunk):
         post(now, "ring%d" % d, ("ring", d, hop, chunk), 0.5 if chunk > 4 else 1.0)
+        order.append(("send", d, hop, chunk))
 
     def share(now, index):
         post(now, "core", ("core", index))
         post(now, "side", ("side", index))
+
+    def release(now, limit):
+        for d in (0, 1):
+            while held[d] and free["ring%d" % d] - now < limit:
+                ring(now, d, *held[d].pop(0))
 
     for d in (0, 1):
         ring(0.0, d, 1, 0)
@@ -51,20 +57,27 @@
     for d in (0, 1):
         ring(0.0, d, 1, 1)
     share(0.0, (0, 0))
-    while heap:
+    order.clear()
+    while heap or held[0] or held[1]:
+        if not heap:
+            release(0.0, float("inf"))
         now, _, key = heapq.heappop(heap)
         order.append(key)
         if key[0] == "pan":
             for d in (0, 1):
-                ring(now, d, 1, key[1] + 2)
+                held[d].append((1, key[1] + 2))
         elif key[0] == "side":
             post(now, "core", ("pass", key[1]))
         elif key[0] == "ring":
             _, d, hop, chunk = key
-            for onward in carried_on(half, full, split, d, hop, chunk):
-                ring(now, d, hop + 1, onward)
+            for onward in carried_on(half, FULL, SPLIT, d, hop, chunk):
+                if onward == 0:
+                    ring(now, d, hop + 1, 0)
+                else:
+                    held[d].append((hop + 1, onward))
             if chunk == 0:
                 share(now, (d, hop))
+        release(now, backlog)
     return order
 
 
@@ -175,8 +188,8 @@
     def handle(key):
         if key[0] == "pan":
             wait_recv(m_part(row, mates[key[1]]), pan_recv.at[key[1]])
-            for d in (0, 1):
-                ring_on(d, 1, key[1] + 2)
+        elif key[0] == "send":
+            ring_on(*key[1:])
         elif key[0] == "side":
             ref, at = g_part(block_row(offset_of(key[1])), side_mate), slot(key[1])
             wait_recv(ref, side_recv.at[at])
@@ -188,8 +201,6 @@
         else:
             _, d, hop, chunk = key
             wait_recv(piece(offset_of((d, hop)), chunk), ring_recv.at[d, hop - 1, chunk])
-            for onward in carried_on(half, FULL, SPLIT, d, hop, chunk):
-                ring_on(d, hop + 1, onward)
             if chunk == 0:
                 share_g((d, hop))
 
@@ -210,7 +221,7 @@
     load_diag = pltpu.make_async_copy(diag, held, load_sem.at[4])
     load_diag.start()
 
-    keys = schedule(half, FULL, SPLIT, 0.78, 1.65, 0.9)
+    keys = schedule(half, 0.78, 1.65, 0.9, 1.0)
     last = [k for k in keys if k[0] == "ring" and k[2] == half and k[3] > 0]
     inert = [k for k in keys if k[0] in ("core", "pass")]
     for key in keys:

time: 27.9 us -> 27.6 us (0.989)
  Pallas kernels: 27.1 us -> 26.8 us
    pallas_call x1, Pallas kernels: 25 us -> 24.6 us  [gathered(): pl.pallas_call(functools.partial(gather_kernel, ring), out_shape=(tall, t...]
where the time goes in v3:
time: 27.6 us; the launch traced here: 27.4 us
  Pallas kernels  26.8 us (97%)
  between operations  0.64 us (2%)
    pallas_call x1, Pallas kernels, gathered(): pl.pallas_call(functools.partial(gather_kernel, ring), out_shape=(tall, t...  24.6 us
    pallas_call x1, Pallas kernels, gathered(): pl.pallas_call(correct_kernel, out_shape=(jax.ShapeDtypeStruct((2, rows,...  2.12 us

profile of v3, /device:TPU:1, one launch (start us, length us, event | category | flops | bytes accessed | tf_op | source)
XLA Modules:
  0.0 27.4 jit_solution(10778112964317702568)
XLA Ops:
  0.6 24.6 %shard_map.59 = (bf16[2,512,512]{2,1,0:T(8,128)(2,1)S(1)}, bf16[2,512,512]{2,1,0:T(8,128)(2,1)S(1)}, f32[2,512,512]{2,1,0:T(8,128)S(1)}) custom-call(s32[1,4]{1,0:T(1,128)} %pattern_hbm.1, bf16[2,64,128]{2,1,0:T(8,128)(2,1)} %inverse.1, bf16[2,16,2048]{2,1,0:T(8,128)(2,1)} %panel.1, f32[2,512,512]{2,1,0:T(8,128)} %diag.1), custom_call_target="tpu_custom_call" | custom-call | tf_op jit(solution)/shard_map/pallas_call | solution.py:326
  25.3 2.1 %shard_map.60 = (bf16[2,64,512]{2,1,0:T(8,128)(2,1)}, f32[2,512,512]{2,1,0:T(8,128)}) custom-call(bf16[2,512,512]{2,1,0:T(8,128)(2,1)S(1)} %get-tuple-element.5.masked, bf16[2,512,512]{2,1,0:T(8,128)(2,1)S(1)} %get-tuple-element.6.coupled, f32[2,512,512]{2,1,0:T(8,128)S(1)} %get-tuple-element.7.held), custom_call_target="tpu_custom_call" | custom-call | tf_op jit(solution)/shard_map/pallas_call | solution.py:349

commit v4 on v3

--- a/solution.py
+++ b/solution.py
@@ -292,7 +292,7 @@
     off[...] = -coupled[:, pl.ds(pl.multiple_of(row * rows, rows), rows), :]
     saves = [pltpu.make_async_copy(off, off_out, save_sem.at[0])]
     saves[0].start()
-    step = min(256, height)
+    step = min(128, height)
     for start in range(0, height, step):
         span = slice(start, start + step)
         for which in (0, 1):
@@ -357,7 +357,7 @@
         scratch_shapes=[
             pltpu.VMEM((2, rows, width), jnp.bfloat16),
             pltpu.VMEM(diag_inverse.shape, jnp.float32),
-            dma((2 * pl.cdiv(height, 256) + 1,)),
+            dma((2 * pl.cdiv(height, 128) + 1,)),
         ],
         compiler_params=pltpu.CompilerParams(vmem_limit_bytes=VMEM_BUDGET),
     )(masked, coupled, held)

time: 27.6 us -> 27.5 us (level)
  no operation moved by 1% of the time
where the time goes in v4:
time: 27.5 us; the launch traced here: 27.4 us
  Pallas kernels  26.7 us (97%)
  between operations  0.64 us (2%)
    pallas_call x1, Pallas kernels, gathered(): pl.pallas_call(functools.partial(gather_kernel, ring), out_shape=(tall, t...  24.6 us
    pallas_call x1, Pallas kernels, gathered(): pl.pallas_call(correct_kernel, out_shape=(jax.ShapeDtypeStruct((2, rows,...  2.08 us

profile of v4, /device:TPU:1, one launch (start us, length us, event | category | flops | bytes accessed | tf_op | source)
XLA Modules:
  0.0 27.4 jit_solution(13721876999636702656)
XLA Ops:
  0.6 24.6 %shard_map.59 = (bf16[2,512,512]{2,1,0:T(8,128)(2,1)S(1)}, bf16[2,512,512]{2,1,0:T(8,128)(2,1)S(1)}, f32[2,512,512]{2,1,0:T(8,128)S(1)}) custom-call(s32[1,4]{1,0:T(1,128)} %pattern_hbm.1, bf16[2,64,128]{2,1,0:T(8,128)(2,1)} %inverse.1, bf16[2,16,2048]{2,1,0:T(8,128)(2,1)} %panel.1, f32[2,512,512]{2,1,0:T(8,128)} %diag.1), custom_call_target="tpu_custom_call" | custom-call | tf_op jit(solution)/shard_map/pallas_call | solution.py:326
  25.3 2.1 %shard_map.60 = (bf16[2,64,512]{2,1,0:T(8,128)(2,1)}, f32[2,512,512]{2,1,0:T(8,128)}) custom-call(bf16[2,512,512]{2,1,0:T(8,128)(2,1)S(1)} %get-tuple-element.5.masked, bf16[2,512,512]{2,1,0:T(8,128)(2,1)S(1)} %get-tuple-element.6.coupled, f32[2,512,512]{2,1,0:T(8,128)S(1)} %get-tuple-element.7.held), custom_call_target="tpu_custom_call" | custom-call | tf_op jit(solution)/shard_map/pallas_call | solution.py:349
